TPU v7x, 32 devices: a whole 2x2x4 slice. The times are simulated.
32 devices in a mesh: dp: 8 (over y, x, core), mp: 4 (over z).
Axes of the slice: x: 2, y: 2, z: 4, core: 2. Of those that a mesh axis runs over, the one named last changes fastest.
Arguments:
- tokens: bfloat16 [6144, 6144], P('dp', 'mp'), may hold values from -6 to 6
- ln_gain: bfloat16 [6144], P('mp'), may hold values from 0.5 to 1.5
- weights: bfloat16 [6144, 12288], P('dp', 'mp'), may hold values from -0.078125 to 0.078125
- grad_partials: bfloat16 [8, 6144, 12288], P('dp', None, 'mp'), may hold values from -40 to 40, as said below
Outputs:
- hidden: bfloat16 [6144, 12288], P('dp', 'mp')
- perturbed_weights: bfloat16 [6144, 12288], P('dp', 'mp')
Inputs may be any that keep to these rules, and one draw needn't show every extreme that they name: `grad_partials`: each slice along the first dimension is one data shard's gradient.
All inputs are finite; a program needn't handle non-finite values.
Results may differ from a plain program's by a relative error of at most 0.012.
Values may be sent and summed in bfloat16 or wider, within the bound.
A program may use at most 192 MiB of HBM per device.

v0:
```python
import functools
import math

import jax
import jax.numpy as jnp
from jax import lax
from jax.experimental import pallas as pl
from jax.experimental.pallas import tpu as pltpu
from jax.sharding import PartitionSpec as P

SUBS = 6
AHEAD = 2
VMEM_LIMIT = 66 * 1000 * 1000


def power_of_two(n):
    return n & (n - 1) == 0


def chip_at(pos, n):
    if not power_of_two(n):
        return pos
    bits = n.bit_length() - 1
    out = 0
    for b in range(bits):
        out = out + ((pos // 2**b + pos // 2 ** (b + 1)) % 2) * 2**b
    return out


def position_of(chip, n):
    if not power_of_two(n):
        return chip
    bits = n.bit_length() - 1
    above, out = 0, 0
    for b in reversed(range(bits)):
        above = (chip // 2**b + above) % 2
        out = out + above * 2**b
    return out


def ring(n):
    me = lax.axis_index("dp")
    chip, core = me // 2, me % 2
    pos = position_of(chip, n)
    right = chip_at((pos + 1) % n, n) * 2 + core
    left = chip_at((pos + n - 1) % n, n) * 2 + core
    return pos, core, (right, left), chip * 2 + 1 - core


def greet(peers):
    barrier = pltpu.get_barrier_semaphore()
    for axis, peer in peers:
        pl.semaphore_signal(
            barrier, inc=1, device_id={axis: peer}, device_id_type=pl.DeviceIdType.MESH
        )
    pl.semaphore_wait(barrier, len(peers))


def others(axis, size):
    me = lax.axis_index(axis)
    return [(axis, (me + k) % size) for k in range(1, size)]


def remote(src, dst, send, recv, peer, axis="dp"):
    return pltpu.make_async_remote_copy(
        src_ref=src,
        dst_ref=dst,
        send_sem=send,
        recv_sem=recv,
        device_id={axis: peer},
        device_id_type=pl.DeviceIdType.MESH,
    )


def scatter_kernel(
    n, n_mp, radius, g_ref, w_ref, gain_ref, out_ref, gains_ref,
    part, recv, own, grad, sq_ref, stat, sums, gains,
    part_send, part_recv, hop_send, hop_recv, own_sem,
    stat_send, stat_recv, sums_send, sums_recv, gain_send, gain_recv,
):
    pos, core, hops, partner = ring(n)
    rows, half = part.shape[2], part.shape[3]
    sub = rows // SUBS
    total = n * SUBS
    tile = 16
    dp_peers, mp_peers = others("dp", 2 * n), others("mp", n_mp)
    greet(dp_peers + mp_peers)

    def block(t, d, which):
        s, i = t // SUBS, t % SUBS
        target = (pos + n - 1 - s + n) % n if d == 0 else (pos + 1 + s) % n
        start = (chip_at(target, n) * 2 + which) * rows + i * sub
        return g_ref.at[pl.ds(pl.multiple_of(start, tile), sub), pl.ds(d * half, half)]

    def piece(ref, t, d):
        return ref.at[t // SUBS, d, pl.ds(pl.multiple_of((t % SUBS) * sub, tile), sub)]

    def push(t, d):
        at = t * 2 + d
        return remote(
            block(t, d, 1 - core), piece(part, t, d), part_send.at[at], part_recv.at[at], partner
        )

    def load(t, d):
        return pltpu.make_async_copy(block(t, d, core), own.at[t % 2, d], own_sem.at[(t % 2) * 2 + d])

    def hop(t, d, src):
        at = t * 2 + d
        return remote(piece(src, t, d), piece(recv, t, d), hop_send.at[at], hop_recv.at[at], hops[d])

    for d in range(2):
        load(0, d).start()

    @pl.loop(0, SUBS)
    def _(t):
        for d in range(2):
            push(t, d).start()

    place = lax.axis_index("mp")
    fetch = pltpu.make_async_copy(w_ref, out_ref, own_sem.at[4])
    fetch.start()
    gain_copies = [
        remote(gain_ref, gains.at[place], gain_send.at[k], gain_recv.at[k], peer, axis)
        for k, (axis, peer) in enumerate(mp_peers)
    ]
    for copy in gain_copies:
        copy.start()
    gains[place] = gain_ref[...]
    sq_ref[...] = jnp.zeros_like(sq_ref)

    def step(t, first, last):
        @pl.when(t + 1 < total)
        def _():
            for d in range(2):
                load(t + 1, d).start()

        @pl.when(t + SUBS < total)
        def _():
            for d in range(2):
                push(t + SUBS, d).start()

        for d in range(2):
            load(t, d).wait()
            push(t, d).wait_recv()
            if not first:
                hop(t - SUBS, d, recv).wait_recv()
            source = piece(part, t, d)
            came = None if first else piece(recv, t - SUBS, d)
            mine = own.at[t % 2, d]

            @pl.loop(0, sub // tile)
            def _(r):
                at = pl.ds(pl.multiple_of(r * tile, tile), tile)
                value = mine[at, :].astype(jnp.float32) + source[at, :].astype(jnp.float32)
                if not first:
                    value = value + came[at, :].astype(jnp.float32)
                if last:
                    row = pl.multiple_of((t % SUBS) * sub + r * tile, tile)
                    grad[pl.ds(row, tile), d * half : (d + 1) * half] = value
                    squared = value * value
                    sq_ref[...] += squared[:8] + squared[8:]
                elif first:
                    source[at, :] = value.astype(jnp.bfloat16)
                else:
                    came[at, :] = value.astype(jnp.bfloat16)

        if not last:
            for d in range(2):
                at = t * 2 + d
                src = piece(part, t, d) if first else piece(recv, t - SUBS, d)
                remote(src, piece(recv, t, d), hop_send.at[at], hop_recv.at[at], hops[d]).start()

    @pl.loop(0, SUBS)
    def _(t):
        step(t, True, False)

    @pl.loop(SUBS, total - SUBS)
    def _(t):
        step(t, False, False)

    @pl.loop(total - SUBS, total)
    def _(t):
        step(t, False, True)

    folded = sq_ref[:, :128]
    for c in range(1, half // 128):
        folded = folded + sq_ref[:, c * 128 : (c + 1) * 128]
    stat[0] = folded

    @pl.loop(0, total)
    def _(t):
        for d in range(2):
            push(t, d).wait_send()

    @pl.loop(0, total - SUBS)
    def _(t):
        for d in range(2):
            hop(t, d, recv).wait_send()

    def share(slots, peers, send, arrive):
        copies = [
            remote(slots.at[0], slots.at[k + 1], send.at[k], arrive.at[k], peer, axis)
            for k, (axis, peer) in enumerate(peers)
        ]
        for copy in copies:
            copy.start()
        for copy in copies:
            copy.wait()
        return jnp.sum(slots[...], axis=0)

    sums[0] = share(stat, dp_peers, stat_send, stat_recv)
    for copy in gain_copies:
        copy.wait()
    gains_ref[...] = gains[...]
    fetch.wait()
    every = share(sums, mp_peers, sums_send, sums_recv)
    squares = jnp.sum(jnp.sum(every, axis=0, keepdims=True), axis=1, keepdims=True)
    scale = radius / jnp.sqrt(squares + 1e-12)

    @pl.loop(0, rows // tile)
    def _(r):
        at = pl.ds(pl.multiple_of(r * tile, tile), tile)
        value = out_ref[at, :].astype(jnp.float32) + scale * grad[at, :]
        out_ref[at, :] = value.astype(jnp.bfloat16)


def reduce_rows(n, n_mp, radius, grads, weights, gain):
    depth, cols = grads.shape
    rows, half = depth // (2 * n), cols // 2
    sub = rows // SUBS
    dma = pltpu.SemaphoreType.DMA
    return pl.pallas_call(
        functools.partial(scatter_kernel, n, n_mp, radius),
        out_shape=(
            jax.ShapeDtypeStruct((rows, cols), jnp.bfloat16),
            jax.ShapeDtypeStruct((n_mp, *gain.shape), jnp.float32),
        ),
        in_specs=[
            pl.BlockSpec(memory_space=pl.ANY),
            pl.BlockSpec(memory_space=pl.ANY),
            pl.BlockSpec(memory_space=pltpu.VMEM),
        ],
        out_specs=(
            pl.BlockSpec(memory_space=pltpu.VMEM),
            pl.BlockSpec(memory_space=pltpu.VMEM),
        ),
        scratch_shapes=[
            pltpu.VMEM((n, 2, rows, half), jnp.bfloat16),
            pltpu.VMEM((n - 1, 2, rows, half), jnp.bfloat16),
            pltpu.VMEM((2, 2, sub, half), jnp.bfloat16),
            pltpu.VMEM((rows, cols), jnp.float32),
            pltpu.VMEM((8, half), jnp.float32),
            pltpu.VMEM((2 * n, 8, 128), jnp.float32),
            pltpu.VMEM((n_mp, 8, 128), jnp.float32),
            pltpu.VMEM((n_mp, *gain.shape), jnp.float32),
            dma((n * SUBS * 2,)),
            dma((n * SUBS * 2,)),
            dma(((n - 1) * SUBS * 2,)),
            dma(((n - 1) * SUBS * 2,)),
            dma((5,)),
            dma((2 * n - 1,)),
            dma((2 * n - 1,)),
            dma((n_mp - 1,)),
            dma((n_mp - 1,)),
            dma((n_mp - 1,)),
            dma((n_mp - 1,)),
        ],
        compiler_params=pltpu.CompilerParams(
            collective_id=1, has_side_effects=True, vmem_limit_bytes=VMEM_LIMIT
        ),
        cost_estimate=pl.CostEstimate(
            flops=200 * 10**9, bytes_accessed=3 * grads.size, transcendentals=0
        ),
        name="reduce_rows",
    )(grads, weights, gain)


def gather_kernel(
    n, x_ref, gain_ref, p_ref, out_ref, normed, buf, pre_ref,
    hop_send, hop_recv, part_send, part_recv, own_sem, x_sem,
):
    pos, core, hops, partner = ring(n)
    rows, width = buf.shape[3] // 2, buf.shape[4]
    half = SUBS * width
    greet([("dp", peer) for peer in (*hops, partner)])

    def mine(i, d):
        return p_ref.at[:, pl.ds(pl.multiple_of(d * half + i * width, 128), width)]

    def piece(s, i, d, which):
        return buf.at[s, d, i, pl.ds(pl.multiple_of(which * rows, 16), rows)]

    def hop(s, i, d, src):
        at = ((s - 1) * SUBS + i) * 2 + d
        return remote(src, piece(s, i, d, core), hop_send.at[at], hop_recv.at[at], hops[d])

    def push(s, i, d, src):
        at = (s * SUBS + i) * 2 + d
        return remote(src, piece(s, i, d, core), part_send.at[at], part_recv.at[at], partner)

    def pushed(s, i, d):
        at = (s * SUBS + i) * 2 + d
        there = piece(s, i, d, 1 - core)
        return remote(there, there, part_send.at[at], part_recv.at[at], partner)

    def keep(i, d):
        return pltpu.make_async_copy(mine(i, d), piece(0, i, d, core), own_sem.at[i * 2 + d])

    fetch = pltpu.make_async_copy(x_ref, normed, x_sem.at[0])
    fetch.start()
    for i in range(AHEAD):
        for d in range(2):
            hop(1, i, d, mine(i, d)).start()

    @pl.loop(0, SUBS)
    def _(i):
        for d in range(2):
            keep(i, d).start()
            push(0, i, d, mine(i, d)).start()

    pre_ref[...] = jnp.zeros_like(pre_ref)
    fetch.wait()

    @pl.loop(0, normed.shape[0] // 16)
    def _(r):
        at = pl.ds(pl.multiple_of(r * 16, 16), 16)
        values = normed[at, :].astype(jnp.float32)
        center = jnp.mean(values, axis=1, keepdims=True)
        moved = values - center
        spread = jnp.mean(moved * moved, axis=1, keepdims=True)
        scaled = moved * (1.0 / jnp.sqrt(spread + 1e-06)) * gain_ref[...]
        normed[at, :] = scaled.astype(jnp.bfloat16)

    def multiply(s, i):
        for d in range(2):
            pushed(s, i, d).wait_recv()
            owner = (pos + n - s) % n if d == 0 else (pos + s) % n
            cols = pl.ds(pl.multiple_of(chip_at(owner, n) * 2 * rows, 128), 2 * rows)
            out = pl.ds(pl.multiple_of(d * half + i * width, 128), width)
            pre_ref[:, out] += jnp.dot(
                normed[:, cols], buf[s, d, i], preferred_element_type=jnp.float32
            )

    def activate(i):
        tall = 64
        for d in range(2):
            cols = pl.ds(pl.multiple_of(d * half + i * width, 128), width)

            @pl.loop(0, pre_ref.shape[0] // tall)
            def _(r):
                at = pl.ds(pl.multiple_of(r * tall, tall), tall)
                pre = pre_ref[at, cols]
                value = 0.5 * pre * (1.0 + lax.erf(pre * math.sqrt(0.5)))
                out_ref[at, cols] = value.astype(jnp.bfloat16)

    @pl.loop(0, SUBS + n - 1)
    def _(wave):
        @pl.when(wave + AHEAD < SUBS)
        def _():
            for d in range(2):
                hop(1, wave + AHEAD, d, mine(wave + AHEAD, d)).start()

        for s in range(1, n):
            i = wave - (s - 1)

            @pl.when((i >= 0) & (i < SUBS))
            def _():
                for d in range(2):
                    hop(s, i, d, piece(s, i, d, core)).wait_recv()
                    if s < n - 1:
                        hop(s + 1, i, d, piece(s, i, d, core)).start()
                    push(s, i, d, piece(s, i, d, core)).start()

            if s == 1:

                @pl.when(wave < SUBS)
                def _():
                    for d in range(2):
                        keep(wave, d).wait()
                    multiply(0, wave)

            @pl.when((i >= 1) & (i <= SUBS))
            def _():
                multiply(s, i - 1)
                if s == n - 1:
                    activate(i - 1)

    @pl.loop(0, SUBS)
    def _(i):
        for d in range(2):
            for s in range(n):
                push(s, i, d, piece(s, i, d, core)).wait_send()
            for s in range(1, n):
                hop(s, i, d, piece(s, i, d, core)).wait_send()


def gather_matmul(n, feats, gains, perturbed):
    tokens, depth = feats.shape
    rows, cols = perturbed.shape
    half = cols // 2
    dma = pltpu.SemaphoreType.DMA
    return pl.pallas_call(
        functools.partial(gather_kernel, n),
        out_shape=jax.ShapeDtypeStruct((tokens, cols), jnp.bfloat16),
        in_specs=[
            pl.BlockSpec(memory_space=pl.ANY),
            pl.BlockSpec(memory_space=pltpu.VMEM),
            pl.BlockSpec(memory_space=pl.ANY),
        ],
        out_specs=pl.BlockSpec(memory_space=pltpu.VMEM),
        scratch_shapes=[
            pltpu.VMEM((tokens, depth), jnp.bfloat16),
            pltpu.VMEM((n, 2, SUBS, 2 * rows, half // SUBS), jnp.bfloat16),
            pltpu.VMEM((tokens, cols), jnp.float32),
            dma(((n - 1) * SUBS * 2,)),
            dma(((n - 1) * SUBS * 2,)),
            dma((n * SUBS * 2,)),
            dma((n * SUBS * 2,)),
            dma((SUBS * 2,)),
            dma((1,)),
        ],
        compiler_params=pltpu.CompilerParams(
            collective_id=2, has_side_effects=True, vmem_limit_bytes=VMEM_LIMIT
        ),
        cost_estimate=pl.CostEstimate(
            flops=2 * tokens * depth * cols,
            bytes_accessed=2 * depth * cols,
            transcendentals=0,
        ),
        name="gather_matmul",
    )(feats, gains, perturbed)


def per_device(n, n_mp, width, tokens, ln_gain, weights, grad_partials):
    feats = lax.all_gather(tokens, "mp", axis=1, tiled=True)
    gain = jnp.broadcast_to(ln_gain.astype(jnp.float32), (8, ln_gain.shape[0]))
    radius = 0.7 * math.sqrt(width)
    perturbed, gains = reduce_rows(n, n_mp, radius, grad_partials[0], weights, gain)
    hidden = gather_matmul(n, feats, gains[:, 0].reshape(1, -1), perturbed)
    return (hidden, perturbed)


def solution(mesh):
    placed = (P("dp", "mp"), P("mp"), P("dp", "mp"), P("dp", None, "mp"))

    def whole(tokens, ln_gain, weights, grad_partials):
        return jax.shard_map(
            functools.partial(per_device, mesh.shape["dp"] // 2, mesh.shape["mp"], weights.shape[1]),
            mesh=mesh,
            in_specs=placed,
            out_specs=(P("dp", "mp"), P("dp", "mp")),
            check_vma=False,
        )(tokens, ln_gain, weights, grad_partials)

    return whole
```

profile of v0, /device:TPU:0, one launch (start us, length us, event | category | flops | bytes accessed | tf_op | source)
XLA Modules:
  0.0 368.4 jit_solution(2411935746292952932)
XLA Ops:
  7.2 0.0 all-gather.2.cloned.1.call-start
  7.2 0.7 all-gather.2.cloned.1.call-update
  7.9 1.3 broadcast_in_dim.3.gain_ref
  9.2 175.2 %reduce_rows.1 = (bf16[768,3072]{1,0:T(8,128)(2,1)}, f32[4,8,1536]{2,1,0:T(8,128)}) custom-call(bf16[6144,3072]{1,0:T(8,128)(2,1)} %bitcast.3, bf16[768,3072]{1,0:T(8,128)(2,1)} %w_ref.1, f32[8,1536]{1,0:T(8,128)} %broadcast_in_dim.3.gain_ref), custom_call_target="tpu_custom_call" | custom-call | flops 199999995904 | bytes 56623104 | tf_op jit(solution)/shard_map/reduce_rows/pallas_call | solution.py:232
  184.5 1.5 slice.3
  186.0 0.0 all-gather.2.cloned.1.call-done.x_ref
  186.0 168.3 %gather_matmul.1 = bf16[768,3072]{1,0:T(8,128)(2,1)} custom-call(bf16[768,6144]{1,0:T(8,128)(2,1)} %all-gather.2.cloned.1.call-done.x_ref, f32[1,6144]{1,0:T(1,128)} %bitcast.2, bf16[768,3072]{1,0:T(8,128)(2,1)} %get-tuple-element.9.p_ref), custom_call_target="tpu_custom_call" | custom-call | flops 28991029248 | bytes 37748736 | tf_op jit(solution)/shard_map/gather_matmul/pallas_call | solution.py:402
  354.3 0.0 copy-start
  354.3 5.0 %copy.8 = bf16[768,3072]{1,0:T(8,128)(2,1)} copy(bf16[768,3072]{1,0:T(8,128)(2,1)} %gather_matmul.1) | data formatting | bytes 9437184
  359.3 0.0 copy-done
  359.3 2.2 copy.9
Async XLA Ops:
  7.2 178.8 %all-gather.2.cloned.1.call-start = ((), (), s32[]{:S(2)}) async-start(), calls=%async_computation | async-start | bytes 11796480 | tf_op jit(solution)/shard_map/all_gather | solution.py:435
  354.3 5.0 %copy-start = (bf16[768,3072]{1,0:T(8,128)(2,1)S(1)}, bf16[768,3072]{1,0:T(8,128)(2,1)}, u32[]{:S(2)}) copy-start(bf16[768,3072]{1,0:T(8,128)(2,1)} %get-tuple-element.9.p_ref) | copy-start | bytes 14155780
Sparse Core Ops, SparseCore 0:
  9.5 169.7 all-gather.1
where the time goes:
time: 369 us; the launch traced here: 368 us
  Pallas kernels  344 us (93%)
  between operations  14.1 us (4%)
  local copies, waits for them, and re-layouts  10.1 us (3%)
    pallas_call x1, Pallas kernels, reduce_rows(): pl.pallas_call(functools.partial(scatter_kernel, n, n_mp, radius), out_sh...  175 us
    pallas_call x1, Pallas kernels, gather_matmul(): pl.pallas_call(functools.partial(gather_kernel, n), out_shape=jax.ShapeDt...  168 us
  transfers between devices with their start and end apart: 1, of which 0 were waited for; matrix products, arithmetic and copies ran while one was open for 1% of the time, Pallas kernels for 48%

commit v1 on v0

--- a/solution.py
+++ b/solution.py
@@ -10,6 +10,8 @@
 
 SUBS = 6
 AHEAD = 2
+CHUNK = 128
+GROUP = 3
 VMEM_LIMIT = 66 * 1000 * 1000
 
 
@@ -47,12 +49,14 @@
     return pos, core, (right, left), chip * 2 + 1 - core
 
 
-def greet(peers):
+def greet(peers, meanwhile=None):
     barrier = pltpu.get_barrier_semaphore()
     for axis, peer in peers:
         pl.semaphore_signal(
             barrier, inc=1, device_id={axis: peer}, device_id_type=pl.DeviceIdType.MESH
         )
+    if meanwhile is not None:
+        meanwhile()
     pl.semaphore_wait(barrier, len(peers))
 
 
@@ -431,13 +435,557 @@
     )(feats, gains, perturbed)
 
 
-def per_device(n, n_mp, width, tokens, ln_gain, weights, grad_partials):
+def ring_program(n, n_mp, radius, tokens, ln_gain, weights, grad_partials):
     feats = lax.all_gather(tokens, "mp", axis=1, tiled=True)
     gain = jnp.broadcast_to(ln_gain.astype(jnp.float32), (8, ln_gain.shape[0]))
-    radius = 0.7 * math.sqrt(width)
     perturbed, gains = reduce_rows(n, n_mp, radius, grad_partials[0], weights, gain)
     hidden = gather_matmul(n, feats, gains[:, 0].reshape(1, -1), perturbed)
     return (hidden, perturbed)
+
+
+def grid_kernel(
+    n_mp, radius, x_ref, gain_ref, g_ref, w_ref, hid_out, w_out,
+    part0, part1, recv0, recv1, own0, own1, grad, sq0, sq1, wnew, hid, near, far,
+    turned, zstat, stat, sums,
+    push_send, push_recv, hop_send, hop_recv, own_sem, load_sem, store_sem,
+    z_send, z_recv, stat_send, stat_recv, sums_send, sums_recv,
+    cross_send, cross_recv, relay_send, relay_recv, spread_send, spread_recv,
+    y_send, y_recv, mine_send, mine_recv, pass_send, pass_recv, c_send, c_recv,
+):
+    part, recv, own, sq = (part0, part1), (recv0, recv1), (own0, own1), (sq0, sq1)
+    me, z = lax.axis_index("dp"), lax.axis_index("mp")
+    core, x, y = me % 2, (me // 2) % 2, me // 4
+    rows, width = part0.shape[1], (part0.shape[2], part1.shape[2])
+    start_col = (0, width[0])
+    sub, tile, tokens, feats = rows // SUBS, 16, hid.shape[0], near.shape[2]
+    chunks = (width[0] // CHUNK, width[1] // CHUNK)
+
+    def device(flip_x, flip_y, which):
+        cx = 1 - x if flip_x else x
+        cy = 1 - y if flip_y else y
+        return (cy * 2 + cx) * 2 + which
+
+    partner, x_peer, y_peer = device(0, 0, 1 - core), device(1, 0, core), device(0, 1, core)
+    flips = (((1, 1), (1, 0), (0, 1), (0, 0)), ((1, 1), (0, 1), (1, 0), (0, 0)))
+    hops = ((x_peer, x_peer, y_peer), (y_peer, y_peer, x_peer))
+    dp_peers, mp_peers = others("dp", 8), others("mp", n_mp)
+
+    def span(i, size):
+        return pl.ds(pl.multiple_of(i * size, size), size)
+
+    def block(s, i, d, which):
+        start = device(*flips[d][s], which) * rows + i * sub
+        return g_ref.at[pl.ds(pl.multiple_of(start, tile), sub), pl.ds(start_col[d], width[d])]
+
+    def piece(ref, s, i):
+        return ref.at[s, span(i, sub)]
+
+    def push(s, i, d):
+        at = (s * SUBS + i) * 2 + d
+        return remote(
+            block(s, i, d, 1 - core), piece(part[d], s, i), push_send.at[at], push_recv.at[at], partner
+        )
+
+    def load(s, i, d, slot):
+        return pltpu.make_async_copy(block(s, i, d, core), own[d].at[slot], own_sem.at[slot * 2 + d])
+
+    def hop(s, i, d):
+        at = (s * SUBS + i) * 2 + d
+        return remote(
+            piece(part[d], s, i), piece(recv[d], s, i), hop_send.at[at], hop_recv.at[at], hops[d][s]
+        )
+
+    def add(s, i, slot):
+        for d in range(2):
+            load(s, i, d, slot).wait()
+            push(s, i, d).wait_recv()
+            came = {0: (), 1: (), 2: (0,), 3: (1, 2)}[s]
+            for k in came:
+                hop(k, i, d).wait_recv()
+            source, mine = piece(part[d], s, i), own[d].at[slot]
+            extra = [piece(recv[d], k, i) for k in came]
+
+            @pl.loop(0, sub // tile)
+            def _(r):
+                at = span(r, tile)
+                value = mine[at, :].astype(jnp.float32) + source[at, :].astype(jnp.float32)
+                for ref in extra:
+                    value = value + ref[at, :].astype(jnp.float32)
+                if s == 3:
+                    row = pl.multiple_of(i * sub + r * tile, tile)
+                    grad[pl.ds(row, tile), start_col[d] : start_col[d] + width[d]] = value
+                    squared = value * value
+                    sq[d][...] += squared[:8] + squared[8:]
+                else:
+                    source[at, :] = value.astype(jnp.bfloat16)
+
+            if s < 3:
+                hop(s, i, d).start()
+
+    def both(make, *args):
+        for d in range(2):
+            make(*args[:2], d, *args[2:]).start()
+
+    fetch = pltpu.make_async_copy(x_ref, hid.at[:, pl.ds(0, feats)], load_sem.at[0])
+    fetch_w = pltpu.make_async_copy(w_ref, wnew, load_sem.at[1])
+    tall, lines = turned.shape[1], 64
+
+    def z_copy(k):
+        return remote(
+            zstat.at[z], zstat.at[z], z_send.at[k], z_recv.at[k], (z + k + 1) % n_mp, "mp"
+        )
+
+    def gather_statistics():
+        fetch.wait()
+
+        @pl.loop(0, tokens // tall)
+        def _(b):
+            @pl.loop(0, tall // lines)
+            def _(r):
+                at = pl.ds(pl.multiple_of(b * tall + r * lines, lines), lines)
+                values = hid[at, :feats].astype(jnp.float32)
+                center = jnp.mean(values, axis=1, keepdims=True)
+                moved = values - center
+                spread = jnp.sum(moved * moved, axis=1, keepdims=True)
+                turned[0, span(r, lines), :] = jnp.broadcast_to(center, (lines, tall))
+                turned[1, span(r, lines), :] = jnp.broadcast_to(spread, (lines, tall))
+
+            for k in range(2):
+                zstat[z, k, b] = turned[k].T[:8]
+
+    belongs = (z + x) % 2 == 0
+    half = tokens // 2
+
+    def cross_copy(send):
+        src = hid.at[pl.ds(0, half), pl.ds(0, feats)] if send == 0 else relay_room
+        return remote(
+            src, far.at[z // 2, pl.ds(send * half, half)], cross_send.at[0], cross_recv.at[0], x_peer
+        )
+
+    relay_room = hid.at[pl.ds(0, half), pl.ds(feats, feats)]
+    relay_copy = remote(
+        hid.at[pl.ds(half, half), pl.ds(0, feats)], relay_room,
+        relay_send.at[0], relay_recv.at[0], z + 1 - 2 * (z % 2), "mp",
+    )
+
+    items = [(x + 2 * k, near.at[k, pl.ds(0, half)]) for k in range(2)]
+    items += [(x + 2 * k, near.at[k, pl.ds(half, half)]) for k in range(2)]
+    items += [(x + 2 * k, far.at[k, pl.ds(0, half)]) for k in range(2)]
+    items += [(1 - x + 2 * k, far.at[k, pl.ds(half, half)]) for k in range(2)]
+    near_top, near_low, far_top, far_low = (0, 1), (2, 3), (4, 5), (6, 7)
+
+    def spread_copy(k, way):
+        return remote(
+            items[k][1], items[k][1], spread_send.at[k * 2 + way], spread_recv.at[k],
+            z + 1 - 2 * way, "mp",
+        )
+
+    def spread(which, steps):
+        for k in which:
+            away = z - items[k][0]
+            if steps == 0 and k >= 4:
+
+                @pl.when(away == 0)
+                def _():
+                    cross_copy(0).wait_recv()
+
+            for way, sign in ((0, 1), (1, -1)):
+                @pl.when((away * sign == steps) & ((z < n_mp - 1) if way == 0 else (z > 0)))
+                def _():
+                    if steps > 0:
+                        spread_copy(k, way).wait_recv()
+                    spread_copy(k, way).start()
+
+    def spread_arrived(which):
+        for k in which:
+            away = z - items[k][0]
+
+            @pl.when(((z == 0) & (away < 0)) | ((z == n_mp - 1) & (away > 0)))
+            def _():
+                spread_copy(k, 0).wait_recv()
+
+    def spread_sent():
+        for k in range(8):
+            away = z - items[k][0]
+
+            @pl.when((away >= 0) & (z < n_mp - 1))
+            def _():
+                spread_copy(k, 0).wait_send()
+
+            @pl.when((away <= 0) & (z > 0))
+            def _():
+                spread_copy(k, 1).wait_send()
+
+        cross_copy(0).wait_send()
+
+        @pl.when((z + x) % 2 == 1)
+        def _():
+            relay_copy.wait_send()
+
+    def normalise():
+        for k in range(n_mp - 1):
+            z_copy(k).wait_recv()
+        centers = [zstat[k, 0] for k in range(n_mp)]
+        center = sum(centers) * (1.0 / n_mp)
+        squared = sum(zstat[k, 1] for k in range(n_mp))
+        squared = squared + feats * sum((one - center) * (one - center) for one in centers)
+        scaled = 1.0 / jnp.sqrt(squared * (1.0 / (feats * n_mp)) + 1e-06)
+        for k in range(n_mp - 1):
+            z_copy(k).wait_send()
+        zstat[0, 0] = center
+        zstat[0, 1] = scaled
+
+        @pl.loop(0, tokens // tall)
+        def _(b):
+            for k in range(2):
+                turned[k] = jnp.broadcast_to(zstat[0, k, b][:1], (tall, tall)).T
+
+            @pl.loop(0, tall // lines)
+            def _(r):
+                at = pl.ds(pl.multiple_of(b * tall + r * lines, lines), lines)
+                values = hid[at, :feats].astype(jnp.float32)
+                moved = values - turned[0, span(r, lines), :1]
+                value = moved * turned[1, span(r, lines), :1] * gain_ref[...].astype(jnp.float32)
+                value = value.astype(jnp.bfloat16)
+                hid[at, :feats] = value
+
+                @pl.when(belongs)
+                def _():
+                    near[z // 2, at, :] = value
+
+        @pl.when((z + x) % 2 == 1)
+        def _():
+            cross_copy(0).start()
+            relay_copy.start()
+
+        spread(near_top + near_low, 0)
+
+    def relay():
+        @pl.when(belongs)
+        def _():
+            relay_copy.wait_recv()
+            cross_copy(1).start()
+
+    def events(i, table):
+        for k, actions in table.items():
+            @pl.when(i == k)
+            def _():
+                for action in actions:
+                    action()
+
+    def later(which, steps):
+        return lambda: spread(which, steps)
+
+    fetch.start()
+    both(load, 0, 0, 0)
+    sq0[...] = jnp.zeros_like(sq0)
+    sq1[...] = jnp.zeros_like(sq1)
+    greet(dp_peers + mp_peers, gather_statistics)
+
+    @pl.loop(0, SUBS)
+    def _(i):
+        both(push, 0, i)
+
+    for k in range(n_mp - 1):
+        z_copy(k).start()
+
+    @pl.loop(0, SUBS)
+    def _(i):
+        @pl.when(i + 1 < SUBS)
+        def _():
+            both(load, 0, i + 1, (i + 1) % 2)
+
+        @pl.when(i + 1 == SUBS)
+        def _():
+            both(load, 1, 0, 0)
+
+        both(push, 1, i)
+        both(push, 2, i)
+        add(0, i, i % 2)
+        events(i, {1: [normalise]})
+
+    @pl.loop(0, SUBS)
+    def _(i):
+        both(load, 2, i, 1)
+        both(push, 3, i)
+        add(1, i, 0)
+
+        @pl.when(i + 1 < SUBS)
+        def _():
+            both(load, 1, i + 1, 0)
+
+        @pl.when(i + 1 == SUBS)
+        def _():
+            both(load, 3, 0, 0)
+
+        add(2, i, 1)
+        events(i, {0: [relay], 3: [later(near_top, 1)]})
+
+    fetch_w.start()
+    spread(far_top, 0)
+    spread(near_low, 1)
+
+    @pl.loop(0, SUBS)
+    def _(i):
+        @pl.when(i + 1 < SUBS)
+        def _():
+            both(load, 3, i + 1, (i + 1) % 2)
+
+        add(3, i, i % 2)
+        events(
+            i,
+            {
+                0: [later(far_low, 0), later(near_top, 2)],
+                1: [later(far_top, 1)],
+                2: [later(far_low, 1)],
+                3: [later(far_top, 2), later(far_low, 2)],
+            },
+        )
+
+    folded = jnp.zeros((8, 128), jnp.float32)
+    for d in range(2):
+        for c in range(width[d] // 128):
+            folded = folded + sq[d][:, c * 128 : (c + 1) * 128]
+    stat[0] = folded
+
+    @pl.loop(0, SUBS)
+    def _(i):
+        for d in range(2):
+            for s in range(4):
+                push(s, i, d).wait_send()
+            for s in range(3):
+                hop(s, i, d).wait_send()
+
+    def share(slots, peers, send, arrive):
+        copies = [
+            remote(slots.at[0], slots.at[k + 1], send.at[k], arrive.at[k], peer, axis)
+            for k, (axis, peer) in enumerate(peers)
+        ]
+        for copy in copies:
+            copy.start()
+        for copy in copies:
+            copy.wait()
+        return jnp.sum(slots[...], axis=0)
+
+    sums[0] = share(stat, dp_peers, stat_send, stat_recv)
+    fetch_w.wait()
+    every = share(sums, mp_peers, sums_send, sums_recv)
+    squares = jnp.sum(jnp.sum(every, axis=0, keepdims=True), axis=1, keepdims=True)
+    scale = radius / jnp.sqrt(squares + 1e-12)
+
+    mine, ours = 2 * y + core, 2 * y + 1 - core
+    theirs, others_there = 2 * (1 - y) + core, 2 * (1 - y) + 1 - core
+
+    def slab(d, slot, j):
+        return part[d].at[slot, :, span(j, CHUNK)]
+
+    def across(d, j):
+        at = d * chunks[0] + j
+        here = slab(d, mine, j)
+        return remote(here, here, y_send.at[at], y_recv.at[at], y_peer)
+
+    def across_arrived(d, j):
+        at = d * chunks[0] + j
+        here = slab(d, theirs, j)
+        return remote(here, here, y_send.at[at], y_recv.at[at], y_peer)
+
+    def give(d, j, slot):
+        at = d * chunks[0] + j
+        here = slab(d, mine if slot == "mine" else theirs, j)
+        sems = (mine_send, mine_recv) if slot == "mine" else (pass_send, pass_recv)
+        return remote(here, here, sems[0].at[at], sems[1].at[at], partner)
+
+    def given(d, j, slot):
+        at = d * chunks[0] + j
+        here = slab(d, ours if slot == "mine" else others_there, j)
+        sems = (mine_send, mine_recv) if slot == "mine" else (pass_send, pass_recv)
+        return remote(here, here, sems[0].at[at], sems[1].at[at], partner)
+
+    def partial_copy(d, j):
+        at = d * chunks[0] + j
+        return remote(
+            recv[d].at[0, :, span(j, CHUNK)], recv[d].at[1, :, span(j, CHUNK)],
+            c_send.at[at], c_recv.at[at], x_peer,
+        )
+
+    def columns(d, j):
+        return pl.ds(pl.multiple_of(start_col[d] + j * CHUNK, 128), CHUNK)
+
+    def hid_store(d, j):
+        at = d * chunks[0] + j
+        cols = columns(d, j)
+        return pltpu.make_async_copy(hid.at[:, cols], hid_out.at[:, cols], store_sem.at[at])
+
+    for d in range(2):
+        @pl.loop(0, chunks[d])
+        def _(j):
+            cols = columns(d, j)
+
+            @pl.loop(0, rows // 64)
+            def _(r):
+                at = span(r, 64)
+                value = wnew[at, cols].astype(jnp.float32) + scale * grad[at, cols]
+                value = value.astype(jnp.bfloat16)
+                wnew[at, cols] = value
+                part[d][mine, at, span(j, CHUNK)] = value
+
+            across(d, j).start()
+            give(d, j, "mine").start()
+
+    keep = pltpu.make_async_copy(wnew, w_out, load_sem.at[2])
+    keep.start()
+
+    def product(left, d, j, size):
+        total = None
+        for k in range(2):
+            right = part[d][2 * k : 2 * k + 2, :, span(j, size)].reshape(2 * rows, size)
+            one = jnp.dot(left[k], right, preferred_element_type=jnp.float32)
+            total = one if total is None else total + one
+        return total
+
+    def arrive(d, j):
+        across_arrived(d, j).wait_recv()
+        give(d, j, "theirs").start()
+
+    def send_far(d, j):
+        given(d, j, "mine").wait_recv()
+        given(d, j, "theirs").wait_recv()
+        recv[d][0, :, span(j, CHUNK)] = product(far, d, j, CHUNK).astype(jnp.bfloat16)
+        partial_copy(d, j).start()
+
+    def keep_near(d, g):
+        size = GROUP * CHUNK
+        cols = pl.ds(pl.multiple_of(start_col[d] + g * size, 128), size)
+        grad[:, cols] = product(near, d, g, size)
+
+    def finish(d, j):
+        cols = columns(d, j)
+        partial_copy(d, j).wait_recv()
+
+        @pl.loop(0, tokens // 64)
+        def _(r):
+            at = span(r, 64)
+            pre = grad[at, cols] + recv[d][1, at, span(j, CHUNK)].astype(jnp.float32)
+            value = 0.5 * pre * (1.0 + lax.erf(pre * math.sqrt(0.5)))
+            hid[at, cols] = value.astype(jnp.bfloat16)
+
+        hid_store(d, j).start()
+
+    spread(near_low, 2)
+    spread_arrived(far_top + far_low)
+
+    @pl.loop(0, chunks[0])
+    def _(j):
+        arrive(0, j)
+        send_far(0, j)
+
+    spread_arrived(near_top + near_low)
+    spread_sent()
+
+    @pl.loop(0, chunks[1])
+    def _(j):
+        arrive(1, j)
+
+        @pl.when(j < chunks[0] // GROUP)
+        def _():
+            keep_near(0, j)
+            for k in range(GROUP):
+                finish(0, j * GROUP + k)
+
+        @pl.when(j >= GROUP)
+        def _():
+            finish(1, j - GROUP)
+
+        send_far(1, j)
+
+        @pl.when(j % GROUP == GROUP - 1)
+        def _():
+            keep_near(1, j // GROUP)
+
+    for j in range(chunks[1] - GROUP, chunks[1]):
+        finish(1, j)
+
+    keep.wait()
+    for d in range(2):
+        @pl.loop(0, chunks[d])
+        def _(j):
+            across(d, j).wait_send()
+            give(d, j, "mine").wait_send()
+            give(d, j, "theirs").wait_send()
+            partial_copy(d, j).wait_send()
+            hid_store(d, j).wait()
+
+
+def grid_program(n_mp, radius, tokens, gain, weights, grads):
+    depth, cols = grads.shape
+    rows = depth // 8
+    count, feats = tokens.shape
+    unit = GROUP * CHUNK
+    first = cols * 3 // 8 // unit * unit
+    wide = (first, cols - first)
+    sub, pieces = rows // SUBS, cols // CHUNK
+    dma = pltpu.SemaphoreType.DMA
+    bf16, f32 = jnp.bfloat16, jnp.float32
+    anywhere = pl.BlockSpec(memory_space=pl.ANY)
+    return pl.pallas_call(
+        functools.partial(grid_kernel, n_mp, radius),
+        out_shape=(
+            jax.ShapeDtypeStruct((count, cols), bf16),
+            jax.ShapeDtypeStruct((rows, cols), bf16),
+        ),
+        in_specs=[anywhere, pl.BlockSpec(memory_space=pltpu.VMEM), anywhere, anywhere],
+        out_specs=(anywhere, anywhere),
+        scratch_shapes=[
+            pltpu.VMEM((4, rows, wide[0]), bf16),
+            pltpu.VMEM((4, rows, wide[1]), bf16),
+            pltpu.VMEM((3, rows, wide[0]), bf16),
+            pltpu.VMEM((3, rows, wide[1]), bf16),
+            pltpu.VMEM((2, sub, wide[0]), bf16),
+            pltpu.VMEM((2, sub, wide[1]), bf16),
+            pltpu.VMEM((rows, cols), f32),
+            pltpu.VMEM((8, wide[0]), f32),
+            pltpu.VMEM((8, wide[1]), f32),
+            pltpu.VMEM((rows, cols), bf16),
+            pltpu.VMEM((count, cols), bf16),
+            pltpu.VMEM((2, count, feats), bf16),
+            pltpu.VMEM((2, count, feats), bf16),
+            pltpu.VMEM((2, 128, 128), f32),
+            pltpu.VMEM((n_mp, 2, count // 128, 8, 128), f32),
+            pltpu.VMEM((8, 8, 128), f32),
+            pltpu.VMEM((n_mp, 8, 128), f32),
+            dma((8 * SUBS,)),
+            dma((8 * SUBS,)),
+            dma((6 * SUBS,)),
+            dma((6 * SUBS,)),
+            dma((4,)),
+            dma((3,)),
+            dma((pieces,)),
+            dma((n_mp - 1,)),
+            dma((n_mp - 1,)),
+            dma((7,)),
+            dma((7,)),
+            dma((n_mp - 1,)),
+            dma((n_mp - 1,)),
+            dma((1,)),
+            dma((1,)),
+            dma((1,)),
+            dma((1,)),
+            dma((16,)),
+            dma((8,)),
+        ]
+        + [dma((pieces,))] * 8,
+        compiler_params=pltpu.CompilerParams(
+            collective_id=3, has_side_effects=True, vmem_limit_bytes=67043328
+        ),
+        name="grid_program",
+    )(tokens, gain, grads, weights)
+
+
+def per_device(n, n_mp, width, tokens, ln_gain, weights, grad_partials):
+    radius = 0.7 * math.sqrt(width)
+    if n == 4 and n_mp == 4 and weights.shape[1] % (8 * GROUP * CHUNK) == 0:
+        return grid_program(n_mp, radius, tokens, ln_gain.reshape(1, -1), weights, grad_partials[0])
+    return ring_program(n, n_mp, radius, tokens, ln_gain, weights, grad_partials)
 
 
 def solution(mesh):

time: 369 us -> 316 us (0.86)
  Pallas kernels: 344 us -> 306 us
  between operations: 14.1 us -> 0.65 us
    pallas_call x2 -> x1, Pallas kernels: 344 us -> 306 us  [grid_program(): pl.pallas_call(functools.partial(grid_kernel, n_mp, radius), out_shape=(j...]
  transfers between devices with their start and end apart: 1 -> 0, of which waited for: 0 -> 0; matrix products, arithmetic and copies ran while one was open for 1% -> 0% of each run, Pallas kernels for 48% -> 0%
where the time goes in v1:
time: 316 us
  Pallas kernels  306 us (97%)
  local copies, waits for them, and re-layouts  8.48 us (3%)
    pallas_call x1, Pallas kernels, grid_program(): pl.pallas_call(functools.partial(grid_kernel, n_mp, radius), out_shape=(j...  306 us
    unnamed x4, local copies, waits for them, and re-layouts  7.2 us

profile of v1, /device:TPU:0, one launch (start us, length us, event | category | flops | bytes accessed | tf_op | source)
XLA Modules:
  0.0 315.6 jit_solution(14520691192011870412)
XLA Ops:
  0.6 1.3 reshape.7.gain_ref
  1.9 306.4 %grid_program.1 = (bf16[768,3072]{1,0:T(8,128)(2,1)}, bf16[768,3072]{1,0:T(8,128)(2,1)}) custom-call(bf16[768,1536]{1,0:T(8,128)(2,1)} %x_ref.1, bf16[1,1536]{1,0:T(2,128)(2,1)} %reshape.7.gain_ref, bf16[6144,3072]{1,0:T(8,128)(2,1)} %bitcast.1, bf16[768,3072]{1,0:T(8,128)(2,1)} %w_ref.1), custom_call_target="tpu_custom_call" | custom-call | tf_op jit(solution)/shard_map/grid_program/pallas_call | solution.py:930
  308.4 0.0 copy-start
  308.4 5.0 %copy.8 = bf16[768,3072]{1,0:T(8,128)(2,1)} copy(bf16[768,3072]{1,0:T(8,128)(2,1)} %get-tuple-element.4) | data formatting | bytes 9437184
  313.4 0.0 copy-done
  313.4 2.2 copy.9
Async XLA Ops:
  308.4 5.0 %copy-start = (bf16[768,3072]{1,0:T(8,128)(2,1)S(1)}, bf16[768,3072]{1,0:T(8,128)(2,1)}, u32[]{:S(2)}) copy-start(bf16[768,3072]{1,0:T(8,128)(2,1)} %get-tuple-element.5) | copy-start | bytes 14155780

commit v2 on v1

--- a/solution.py
+++ b/solution.py
@@ -49,14 +49,12 @@
     return pos, core, (right, left), chip * 2 + 1 - core
 
 
-def greet(peers, meanwhile=None):
+def greet(peers):
     barrier = pltpu.get_barrier_semaphore()
-    for axis, peer in peers:
+    for device_id in peers:
         pl.semaphore_signal(
-            barrier, inc=1, device_id={axis: peer}, device_id_type=pl.DeviceIdType.MESH
+            barrier, inc=1, device_id=device_id, device_id_type=pl.DeviceIdType.MESH
         )
-    if meanwhile is not None:
-        meanwhile()
     pl.semaphore_wait(barrier, len(peers))
 
 
@@ -88,7 +86,7 @@
     total = n * SUBS
     tile = 16
     dp_peers, mp_peers = others("dp", 2 * n), others("mp", n_mp)
-    greet(dp_peers + mp_peers)
+    greet([{axis: peer} for axis, peer in dp_peers + mp_peers])
 
     def block(t, d, which):
         s, i = t // SUBS, t % SUBS
@@ -286,7 +284,7 @@
     pos, core, hops, partner = ring(n)
     rows, width = buf.shape[3] // 2, buf.shape[4]
     half = SUBS * width
-    greet([("dp", peer) for peer in (*hops, partner)])
+    greet([{"dp": peer} for peer in (*hops, partner)])
 
     def mine(i, d):
         return p_ref.at[:, pl.ds(pl.multiple_of(d * half + i * width, 128), width)]
@@ -444,11 +442,11 @@
 
 
 def grid_kernel(
-    n_mp, radius, x_ref, gain_ref, g_ref, w_ref, hid_out, w_out,
-    part0, part1, recv0, recv1, own0, own1, grad, sq0, sq1, wnew, hid, near, far,
-    turned, zstat, stat, sums,
-    push_send, push_recv, hop_send, hop_recv, own_sem, load_sem, store_sem,
-    z_send, z_recv, stat_send, stat_recv, sums_send, sums_recv,
+    n_mp, radius, x_ref, gain_ref, g_ref, w_ref, hid, wnew,
+    part0, part1, recv0, recv1, own0, own1, grad, sq0, sq1, near, far,
+    turned, zstat, stat,
+    push_send, push_recv, hop_send, hop_recv, own_sem, load_sem,
+    z_send, z_recv, stat_send, stat_recv,
     cross_send, cross_recv, relay_send, relay_recv, spread_send, spread_recv,
     y_send, y_recv, mine_send, mine_recv, pass_send, pass_recv, c_send, c_recv,
 ):
@@ -468,7 +466,9 @@
     partner, x_peer, y_peer = device(0, 0, 1 - core), device(1, 0, core), device(0, 1, core)
     flips = (((1, 1), (1, 0), (0, 1), (0, 0)), ((1, 1), (0, 1), (1, 0), (0, 0)))
     hops = ((x_peer, x_peer, y_peer), (y_peer, y_peer, x_peer))
-    dp_peers, mp_peers = others("dp", 8), others("mp", n_mp)
+    everyone = [
+        {"dp": (me + a) % 8, "mp": (z + b) % n_mp} for a in range(8) for b in range(n_mp) if a + b
+    ]
 
     def span(i, size):
         return pl.ds(pl.multiple_of(i * size, size), size)
@@ -483,7 +483,7 @@
     def push(s, i, d):
         at = (s * SUBS + i) * 2 + d
         return remote(
-            block(s, i, d, 1 - core), piece(part[d], s, i), push_send.at[at], push_recv.at[at], partner
+            block(s, i, d, 1 - core), piece(part[d], s, i), push_send.at[d], push_recv.at[at], partner
         )
 
     def load(s, i, d, slot):
@@ -492,7 +492,7 @@
     def hop(s, i, d):
         at = (s * SUBS + i) * 2 + d
         return remote(
-            piece(part[d], s, i), piece(recv[d], s, i), hop_send.at[at], hop_recv.at[at], hops[d][s]
+            piece(part[d], s, i), piece(recv[d], s, i), hop_send.at[d], hop_recv.at[at], hops[d][s]
         )
 
     def add(s, i, slot):
@@ -500,8 +500,8 @@
             load(s, i, d, slot).wait()
             push(s, i, d).wait_recv()
             came = {0: (), 1: (), 2: (0,), 3: (1, 2)}[s]
-            for k in came:
-                hop(k, i, d).wait_recv()
+            if s > 1:
+                hop(2 * s - 4, i, d).wait_recv()
             source, mine = piece(part[d], s, i), own[d].at[slot]
             extra = [piece(recv[d], k, i) for k in came]
 
@@ -553,6 +553,9 @@
             for k in range(2):
                 zstat[z, k, b] = turned[k].T[:8]
 
+        for k in range(n_mp - 1):
+            z_copy(k).start()
+
     belongs = (z + x) % 2 == 0
     half = tokens // 2
 
@@ -568,11 +571,11 @@
         relay_send.at[0], relay_recv.at[0], z + 1 - 2 * (z % 2), "mp",
     )
 
-    items = [(x + 2 * k, near.at[k, pl.ds(0, half)]) for k in range(2)]
-    items += [(x + 2 * k, near.at[k, pl.ds(half, half)]) for k in range(2)]
+    ends = ((3 * x, x), (2 - x, 1 - x))
+    items = [(o, near.at[k, pl.ds(h * half, half)]) for o, k in ends for h in range(2)]
     items += [(x + 2 * k, far.at[k, pl.ds(0, half)]) for k in range(2)]
     items += [(1 - x + 2 * k, far.at[k, pl.ds(half, half)]) for k in range(2)]
-    near_top, near_low, far_top, far_low = (0, 1), (2, 3), (4, 5), (6, 7)
+    near_top, long_low, short_low, far_top, far_low = (0, 2), (1,), (3,), (4, 5), (6, 7)
 
     def spread_copy(k, way):
         return remote(
@@ -635,30 +638,30 @@
         zstat[0, 0] = center
         zstat[0, 1] = scaled
 
-        @pl.loop(0, tokens // tall)
-        def _(b):
-            for k in range(2):
-                turned[k] = jnp.broadcast_to(zstat[0, k, b][:1], (tall, tall)).T
-
-            @pl.loop(0, tall // lines)
-            def _(r):
-                at = pl.ds(pl.multiple_of(b * tall + r * lines, lines), lines)
-                values = hid[at, :feats].astype(jnp.float32)
-                moved = values - turned[0, span(r, lines), :1]
-                value = moved * turned[1, span(r, lines), :1] * gain_ref[...].astype(jnp.float32)
-                value = value.astype(jnp.bfloat16)
-                hid[at, :feats] = value
-
-                @pl.when(belongs)
-                def _():
-                    near[z // 2, at, :] = value
-
-        @pl.when((z + x) % 2 == 1)
-        def _():
-            cross_copy(0).start()
-            relay_copy.start()
-
-        spread(near_top + near_low, 0)
+        for h in range(2):
+            @pl.loop(h * half // tall, (h + 1) * half // tall)
+            def _(b):
+                for k in range(2):
+                    turned[k] = jnp.broadcast_to(zstat[0, k, b][:1], (tall, tall)).T
+
+                @pl.loop(0, tall // lines)
+                def _(r):
+                    at = pl.ds(pl.multiple_of(b * tall + r * lines, lines), lines)
+                    values = hid[at, :feats].astype(jnp.float32)
+                    moved = values - turned[0, span(r, lines), :1]
+                    value = moved * turned[1, span(r, lines), :1] * gain_ref[...].astype(jnp.float32).reshape(1, feats)
+                    value = value.astype(jnp.bfloat16)
+                    hid[at, :feats] = value
+
+                    @pl.when(belongs)
+                    def _():
+                        near[z // 2, at, :] = value
+
+            @pl.when((z + x) % 2 == 1)
+            def _():
+                (cross_copy(0) if h == 0 else relay_copy).start()
+
+            spread(near_top if h == 0 else long_low + short_low, 0)
 
     def relay():
         @pl.when(belongs)
@@ -680,15 +683,12 @@
     both(load, 0, 0, 0)
     sq0[...] = jnp.zeros_like(sq0)
     sq1[...] = jnp.zeros_like(sq1)
-    greet(dp_peers + mp_peers, gather_statistics)
+    greet(everyone)
 
     @pl.loop(0, SUBS)
     def _(i):
         both(push, 0, i)
 
-    for k in range(n_mp - 1):
-        z_copy(k).start()
-
     @pl.loop(0, SUBS)
     def _(i):
         @pl.when(i + 1 < SUBS)
@@ -702,7 +702,7 @@
         both(push, 1, i)
         both(push, 2, i)
         add(0, i, i % 2)
-        events(i, {1: [normalise]})
+        events(i, {0: [gather_statistics], 2: [normalise]})
 
     @pl.loop(0, SUBS)
     def _(i):
@@ -719,11 +719,17 @@
             both(load, 3, 0, 0)
 
         add(2, i, 1)
-        events(i, {0: [relay], 3: [later(near_top, 1)]})
+        events(
+            i,
+            {
+                0: [relay],
+                2: [later(near_top, 1)],
+                3: [later(far_top, 0)],
+                4: [later(short_low, 1)],
+            },
+        )
 
     fetch_w.start()
-    spread(far_top, 0)
-    spread(near_low, 1)
 
     @pl.loop(0, SUBS)
     def _(i):
@@ -731,16 +737,17 @@
         def _():
             both(load, 3, i + 1, (i + 1) % 2)
 
-        add(3, i, i % 2)
+        for d in range(2):
+            hop(1, i, d).wait_recv()
         events(
             i,
             {
-                0: [later(far_low, 0), later(near_top, 2)],
-                1: [later(far_top, 1)],
-                2: [later(far_low, 1)],
+                0: [later(near_top, 2), later(far_low, 0)],
                 3: [later(far_top, 2), later(far_low, 2)],
             },
         )
+        add(3, i, i % 2)
+        events(i, {0: [later(far_top, 1)], 1: [later(far_low, 1)], 2: [later(long_low, 1)]})
 
     folded = jnp.zeros((8, 128), jnp.float32)
     for d in range(2):
@@ -748,28 +755,27 @@
             folded = folded + sq[d][:, c * 128 : (c + 1) * 128]
     stat[0] = folded
 
-    @pl.loop(0, SUBS)
-    def _(i):
-        for d in range(2):
-            for s in range(4):
-                push(s, i, d).wait_send()
-            for s in range(3):
-                hop(s, i, d).wait_send()
-
-    def share(slots, peers, send, arrive):
-        copies = [
-            remote(slots.at[0], slots.at[k + 1], send.at[k], arrive.at[k], peer, axis)
-            for k, (axis, peer) in enumerate(peers)
-        ]
-        for copy in copies:
-            copy.start()
-        for copy in copies:
-            copy.wait()
-        return jnp.sum(slots[...], axis=0)
-
-    sums[0] = share(stat, dp_peers, stat_send, stat_recv)
+    for d in range(2):
+        remote(part[d], part[d], push_send.at[d], push_recv.at[0], partner).wait_send()
+        sent = part[d].at[pl.ds(0, 3)]
+        remote(sent, recv[d], hop_send.at[d], hop_recv.at[0], partner).wait_send()
+
+    def shared(src, dst, device_id):
+        return pltpu.make_async_remote_copy(
+            src_ref=src,
+            dst_ref=dst,
+            send_sem=stat_send.at[0],
+            recv_sem=stat_recv.at[0],
+            device_id=device_id,
+            device_id_type=pl.DeviceIdType.MESH,
+        )
+
+    for k, device_id in enumerate(everyone):
+        shared(stat.at[pl.ds(0, 1)], stat.at[pl.ds(k + 1, 1)], device_id).start()
     fetch_w.wait()
-    every = share(sums, mp_peers, sums_send, sums_recv)
+    rest = stat.at[pl.ds(1, len(everyone))]
+    shared(rest, rest, everyone[0]).wait()
+    every = jnp.sum(stat[...], axis=0)
     squares = jnp.sum(jnp.sum(every, axis=0, keepdims=True), axis=1, keepdims=True)
     scale = radius / jnp.sqrt(squares + 1e-12)
 
@@ -782,39 +788,34 @@
     def across(d, j):
         at = d * chunks[0] + j
         here = slab(d, mine, j)
-        return remote(here, here, y_send.at[at], y_recv.at[at], y_peer)
+        return remote(here, here, y_send.at[d], y_recv.at[at], y_peer)
 
     def across_arrived(d, j):
         at = d * chunks[0] + j
         here = slab(d, theirs, j)
-        return remote(here, here, y_send.at[at], y_recv.at[at], y_peer)
+        return remote(here, here, y_send.at[d], y_recv.at[at], y_peer)
 
     def give(d, j, slot):
         at = d * chunks[0] + j
         here = slab(d, mine if slot == "mine" else theirs, j)
         sems = (mine_send, mine_recv) if slot == "mine" else (pass_send, pass_recv)
-        return remote(here, here, sems[0].at[at], sems[1].at[at], partner)
+        return remote(here, here, sems[0].at[d], sems[1].at[at], partner)
 
     def given(d, j, slot):
         at = d * chunks[0] + j
         here = slab(d, ours if slot == "mine" else others_there, j)
         sems = (mine_send, mine_recv) if slot == "mine" else (pass_send, pass_recv)
-        return remote(here, here, sems[0].at[at], sems[1].at[at], partner)
+        return remote(here, here, sems[0].at[d], sems[1].at[at], partner)
 
     def partial_copy(d, j):
         at = d * chunks[0] + j
         return remote(
             recv[d].at[0, :, span(j, CHUNK)], recv[d].at[1, :, span(j, CHUNK)],
-            c_send.at[at], c_recv.at[at], x_peer,
+            c_send.at[d], c_recv.at[at], x_peer,
         )
 
     def columns(d, j):
         return pl.ds(pl.multiple_of(start_col[d] + j * CHUNK, 128), CHUNK)
-
-    def hid_store(d, j):
-        at = d * chunks[0] + j
-        cols = columns(d, j)
-        return pltpu.make_async_copy(hid.at[:, cols], hid_out.at[:, cols], store_sem.at[at])
 
     for d in range(2):
         @pl.loop(0, chunks[d])
@@ -832,14 +833,11 @@
             across(d, j).start()
             give(d, j, "mine").start()
 
-    keep = pltpu.make_async_copy(wnew, w_out, load_sem.at[2])
-    keep.start()
-
-    def product(left, d, j, size):
+    def product(left, at, d, j, size):
         total = None
         for k in range(2):
             right = part[d][2 * k : 2 * k + 2, :, span(j, size)].reshape(2 * rows, size)
-            one = jnp.dot(left[k], right, preferred_element_type=jnp.float32)
+            one = jnp.dot(left[k, at], right, preferred_element_type=jnp.float32)
             total = one if total is None else total + one
         return total
 
@@ -850,13 +848,20 @@
     def send_far(d, j):
         given(d, j, "mine").wait_recv()
         given(d, j, "theirs").wait_recv()
-        recv[d][0, :, span(j, CHUNK)] = product(far, d, j, CHUNK).astype(jnp.bfloat16)
+        recv[d][0, :, span(j, CHUNK)] = product(far, pl.ds(0, tokens), d, j, CHUNK).astype(jnp.bfloat16)
         partial_copy(d, j).start()
 
-    def keep_near(d, g):
-        size = GROUP * CHUNK
+    def keep_near(d, g, h):
+        size, at = GROUP * CHUNK, pl.ds(h * half, half)
         cols = pl.ds(pl.multiple_of(start_col[d] + g * size, 128), size)
-        grad[:, cols] = product(near, d, g, size)
+        grad[at, cols] = product(near, at, d, g, size)
+
+    def settle(d):
+        here, there, partial = part[d].at[mine], part[d].at[theirs], recv[d].at[0]
+        remote(here, here, y_send.at[d], y_recv.at[0], y_peer).wait_send()
+        remote(here, here, mine_send.at[d], mine_recv.at[0], partner).wait_send()
+        remote(there, there, pass_send.at[d], pass_recv.at[0], partner).wait_send()
+        remote(partial, partial, c_send.at[d], c_recv.at[0], x_peer).wait_send()
 
     def finish(d, j):
         cols = columns(d, j)
@@ -869,9 +874,7 @@
             value = 0.5 * pre * (1.0 + lax.erf(pre * math.sqrt(0.5)))
             hid[at, cols] = value.astype(jnp.bfloat16)
 
-        hid_store(d, j).start()
-
-    spread(near_low, 2)
+    spread(long_low, 2)
     spread_arrived(far_top + far_low)
 
     @pl.loop(0, chunks[0])
@@ -879,41 +882,48 @@
         arrive(0, j)
         send_far(0, j)
 
-    spread_arrived(near_top + near_low)
+    spread_arrived(near_top + long_low + short_low)
+    groups = (chunks[0] // GROUP, chunks[1] // GROUP)
+    turns = [0, 1] + [1 + GROUP * k for k in range(1, 2 * groups[0] - 1)]
     spread_sent()
 
     @pl.loop(0, chunks[1])
     def _(j):
         arrive(1, j)
 
-        @pl.when(j < chunks[0] // GROUP)
-        def _():
-            keep_near(0, j)
+        @pl.when(j > GROUP)
+        def _():
+            finish(1, j - GROUP - 1)
+
+        for g in range(groups[0]):
             for k in range(GROUP):
-                finish(0, j * GROUP + k)
-
-        @pl.when(j >= GROUP)
-        def _():
-            finish(1, j - GROUP)
+                @pl.when(j == turns[2 * g + 1] + 1 + k)
+                def _():
+                    finish(0, g * GROUP + k)
 
         send_far(1, j)
 
         @pl.when(j % GROUP == GROUP - 1)
         def _():
-            keep_near(1, j // GROUP)
-
-    for j in range(chunks[1] - GROUP, chunks[1]):
+            keep_near(1, j // GROUP, 0)
+
+        @pl.when((j % GROUP == 0) & (j > 0))
+        def _():
+            keep_near(1, j // GROUP - 1, 1)
+
+        for k, turn in enumerate(turns):
+            @pl.when(j == turn)
+            def _():
+                keep_near(0, k // 2, k % 2)
+
+    keep_near(1, groups[1] - 1, 1)
+    for j in range(max(chunks[1] - turns[-1] - 1, 0), GROUP):
+        finish(0, chunks[0] - GROUP + j)
+    for j in range(chunks[1] - GROUP - 1, chunks[1]):
         finish(1, j)
 
-    keep.wait()
     for d in range(2):
-        @pl.loop(0, chunks[d])
-        def _(j):
-            across(d, j).wait_send()
-            give(d, j, "mine").wait_send()
-            give(d, j, "theirs").wait_send()
-            partial_copy(d, j).wait_send()
-            hid_store(d, j).wait()
+        settle(d)
 
 
 def grid_program(n_mp, radius, tokens, gain, weights, grads):
@@ -930,11 +940,11 @@
     return pl.pallas_call(
         functools.partial(grid_kernel, n_mp, radius),
         out_shape=(
-            jax.ShapeDtypeStruct((count, cols), bf16),
-            jax.ShapeDtypeStruct((rows, cols), bf16),
+            pltpu.VMEM((count, cols), bf16),
+            pltpu.VMEM((rows, cols), bf16),
         ),
         in_specs=[anywhere, pl.BlockSpec(memory_space=pltpu.VMEM), anywhere, anywhere],
-        out_specs=(anywhere, anywhere),
+        out_specs=(pl.BlockSpec(memory_space=pltpu.VMEM), pl.BlockSpec(memory_space=pltpu.VMEM)),
         scratch_shapes=[
             pltpu.VMEM((4, rows, wide[0]), bf16),
             pltpu.VMEM((4, rows, wide[1]), bf16),
@@ -945,27 +955,21 @@
             pltpu.VMEM((rows, cols), f32),
             pltpu.VMEM((8, wide[0]), f32),
             pltpu.VMEM((8, wide[1]), f32),
-            pltpu.VMEM((rows, cols), bf16),
-            pltpu.VMEM((count, cols), bf16),
             pltpu.VMEM((2, count, feats), bf16),
             pltpu.VMEM((2, count, feats), bf16),
             pltpu.VMEM((2, 128, 128), f32),
             pltpu.VMEM((n_mp, 2, count // 128, 8, 128), f32),
-            pltpu.VMEM((8, 8, 128), f32),
-            pltpu.VMEM((n_mp, 8, 128), f32),
+            pltpu.VMEM((8 * n_mp, 8, 128), f32),
+            dma((2,)),
             dma((8 * SUBS,)),
-            dma((8 * SUBS,)),
-            dma((6 * SUBS,)),
+            dma((2,)),
             dma((6 * SUBS,)),
             dma((4,)),
-            dma((3,)),
-            dma((pieces,)),
+            dma((2,)),
             dma((n_mp - 1,)),
             dma((n_mp - 1,)),
-            dma((7,)),
-            dma((7,)),
-            dma((n_mp - 1,)),
-            dma((n_mp - 1,)),
+            dma((1,)),
+            dma((1,)),
             dma((1,)),
             dma((1,)),
             dma((1,)),
@@ -973,9 +977,9 @@
             dma((16,)),
             dma((8,)),
         ]
-        + [dma((pieces,))] * 8,
+        + [dma((2,)), dma((pieces,))] * 4,
         compiler_params=pltpu.CompilerParams(
-            collective_id=3, has_side_effects=True, vmem_limit_bytes=67043328
+            collective_id=3, has_side_effects=True, vmem_limit_bytes=57000000
         ),
         name="grid_program",
     )(tokens, gain, grads, weights)
@@ -984,7 +988,7 @@
 def per_device(n, n_mp, width, tokens, ln_gain, weights, grad_partials):
     radius = 0.7 * math.sqrt(width)
     if n == 4 and n_mp == 4 and weights.shape[1] % (8 * GROUP * CHUNK) == 0:
-        return grid_program(n_mp, radius, tokens, ln_gain.reshape(1, -1), weights, grad_partials[0])
+        return grid_program(n_mp, radius, tokens, ln_gain, weights, grad_partials[0])
     return ring_program(n, n_mp, radius, tokens, ln_gain, weights, grad_partials)
 
 

time: 316 us -> 303 us (0.959)
  Pallas kernels: 306 us -> 297 us
  local copies, waits for them, and re-layouts: 8.48 us -> 4.37 us
    pallas_call x1, Pallas kernels: 306 us -> 297 us  [grid_program(): pl.pallas_call(functools.partial(grid_kernel, n_mp, radius), out_shape=(p...]
    unnamed x4 -> x2, local copies, waits for them, and re-layouts: 7.2 us -> 4.37 us
where the time goes in v2:
time: 303 us; the launch traced here: 302 us
  Pallas kernels  297 us (98%)
  local copies, waits for them, and re-layouts  4.37 us (1%)
    pallas_call x1, Pallas kernels, grid_program(): pl.pallas_call(functools.partial(grid_kernel, n_mp, radius), out_shape=(p...  297 us

profile of v2, /device:TPU:0, one launch (start us, length us, event | category | flops | bytes accessed | tf_op | source)
XLA Modules:
  0.0 302.2 jit_solution(16558094116596130867)
XLA Ops:
  0.6 297.2 %grid_program.1 = (bf16[768,3072]{1,0:T(8,128)(2,1)S(1)}, bf16[768,3072]{1,0:T(8,128)(2,1)S(1)}) custom-call(bf16[768,1536]{1,0:T(8,128)(2,1)} %x_ref.1, bf16[1536]{0:T(1024)(128)(2,1)} %gain_ref.1, bf16[6144,3072]{1,0:T(8,128)(2,1)} %bitcast.1, bf16[768,3072]{1,0:T(8,128)(2,1)} %w_ref.1), custom_call_target="tpu_custom_call" | custom-call | tf_op jit(solution)/shard_map/grid_program/pallas_call | solution.py:940
  297.8 2.2 copy.8
  300.0 2.2 copy.9

commit v3 on v2

--- a/solution.py
+++ b/solution.py
@@ -12,6 +12,7 @@
 AHEAD = 2
 CHUNK = 128
 GROUP = 3
+STRIPS = 2
 VMEM_LIMIT = 66 * 1000 * 1000
 
 
@@ -444,11 +445,12 @@
 def grid_kernel(
     n_mp, radius, x_ref, gain_ref, g_ref, w_ref, hid, wnew,
     part0, part1, recv0, recv1, own0, own1, grad, sq0, sq1, near, far,
-    turned, zstat, stat,
+    turned, zstat, stat, lead, landed,
     push_send, push_recv, hop_send, hop_recv, own_sem, load_sem,
     z_send, z_recv, stat_send, stat_recv,
     cross_send, cross_recv, relay_send, relay_recv, spread_send, spread_recv,
     y_send, y_recv, mine_send, mine_recv, pass_send, pass_recv, c_send, c_recv,
+    head_send, head_recv,
 ):
     part, recv, own, sq = (part0, part1), (recv0, recv1), (own0, own1), (sq0, sq1)
     me, z = lax.axis_index("dp"), lax.axis_index("mp")
@@ -469,6 +471,9 @@
     everyone = [
         {"dp": (me + a) % 8, "mp": (z + b) % n_mp} for a in range(8) for b in range(n_mp) if a + b
     ]
+
+    mine, ours = 2 * y + core, 2 * y + 1 - core
+    theirs, others_there = 2 * (1 - y) + core, 2 * (1 - y) + 1 - core
 
     def span(i, size):
         return pl.ds(pl.multiple_of(i * size, size), size)
@@ -773,14 +778,24 @@
     for k, device_id in enumerate(everyone):
         shared(stat.at[pl.ds(0, 1)], stat.at[pl.ds(k + 1, 1)], device_id).start()
     fetch_w.wait()
+
+    top = rows // 2
+
+    def head(k):
+        here = part0.at[mine, pl.ds(top, top), pl.ds(0, CHUNK)]
+        src = (wnew.at[pl.ds(0, top), pl.ds(0, CHUNK)], lead, here)[k]
+        dst = (landed.at[0], landed.at[1], here)[k]
+        return remote(src, dst, head_send.at[k], head_recv.at[k], y_peer)
+
+    head(0).start()
+    lead[...] = grad[:top, :CHUNK].astype(jnp.bfloat16)
+    head(1).start()
     rest = stat.at[pl.ds(1, len(everyone))]
     shared(rest, rest, everyone[0]).wait()
     every = jnp.sum(stat[...], axis=0)
     squares = jnp.sum(jnp.sum(every, axis=0, keepdims=True), axis=1, keepdims=True)
     scale = radius / jnp.sqrt(squares + 1e-12)
 
-    mine, ours = 2 * y + core, 2 * y + 1 - core
-    theirs, others_there = 2 * (1 - y) + core, 2 * (1 - y) + 1 - core
 
     def slab(d, slot, j):
         return part[d].at[slot, :, span(j, CHUNK)]
@@ -817,21 +832,48 @@
     def columns(d, j):
         return pl.ds(pl.multiple_of(start_col[d] + j * CHUNK, 128), CHUNK)
 
+    def perturb(d, j):
+        cols = columns(d, j)
+
+        @pl.loop(0, rows // 256)
+        def _(r):
+            at = span(r, 256)
+            value = wnew[at, cols].astype(jnp.float32) + scale * grad[at, cols]
+            value = value.astype(jnp.bfloat16)
+            wnew[at, cols] = value
+            part[d][mine, at, span(j, CHUNK)] = value
+
+    for k in range(2):
+        head(k).wait_send()
+    perturb(0, 0)
+    head(2).start()
+    give(0, 0, "mine").start()
     for d in range(2):
-        @pl.loop(0, chunks[d])
+        @pl.loop(1 - d, chunks[d])
         def _(j):
-            cols = columns(d, j)
-
-            @pl.loop(0, rows // 64)
-            def _(r):
-                at = span(r, 64)
-                value = wnew[at, cols].astype(jnp.float32) + scale * grad[at, cols]
-                value = value.astype(jnp.bfloat16)
-                wnew[at, cols] = value
-                part[d][mine, at, span(j, CHUNK)] = value
-
+            perturb(d, j)
             across(d, j).start()
-            give(d, j, "mine").start()
+
+    def give_next(d, j):
+        @pl.when(j + 1 < chunks[d])
+        def _():
+            give(d, j + 1, "mine").start()
+
+        if d == 0:
+
+            @pl.when(j + 1 == chunks[0])
+            def _():
+                give(1, 0, "mine").start()
+
+    def arrive_first():
+        for k in range(2):
+            head(k).wait_recv()
+        value = landed[0].astype(jnp.float32) + scale * landed[1].astype(jnp.float32)
+        part0[theirs, :top, :CHUNK] = value.astype(jnp.bfloat16)
+        there = part0.at[theirs, pl.ds(top, top), pl.ds(0, CHUNK)]
+        remote(there, there, head_send.at[2], head_recv.at[2], y_peer).wait_recv()
+        give(0, 0, "theirs").start()
+        give_next(0, 0)
 
     def product(left, at, d, j, size):
         total = None
@@ -844,6 +886,7 @@
     def arrive(d, j):
         across_arrived(d, j).wait_recv()
         give(d, j, "theirs").start()
+        give_next(d, j)
 
     def send_far(d, j):
         given(d, j, "mine").wait_recv()
@@ -858,7 +901,9 @@
 
     def settle(d):
         here, there, partial = part[d].at[mine], part[d].at[theirs], recv[d].at[0]
-        remote(here, here, y_send.at[d], y_recv.at[0], y_peer).wait_send()
+        first = CHUNK * (1 - d)
+        sent = part[d].at[mine, :, pl.ds(first, width[d] - first)]
+        remote(sent, sent, y_send.at[d], y_recv.at[0], y_peer).wait_send()
         remote(here, here, mine_send.at[d], mine_recv.at[0], partner).wait_send()
         remote(there, there, pass_send.at[d], pass_recv.at[0], partner).wait_send()
         remote(partial, partial, c_send.at[d], c_recv.at[0], x_peer).wait_send()
@@ -877,7 +922,10 @@
     spread(long_low, 2)
     spread_arrived(far_top + far_low)
 
-    @pl.loop(0, chunks[0])
+    arrive_first()
+    send_far(0, 0)
+
+    @pl.loop(1, chunks[0])
     def _(j):
         arrive(0, j)
         send_far(0, j)
@@ -922,8 +970,40 @@
     for j in range(chunks[1] - GROUP - 1, chunks[1]):
         finish(1, j)
 
+    head(2).wait_send()
     for d in range(2):
         settle(d)
+
+
+def store_kernel(hid, weights, hid_out, w_out, sem):
+    strip = hid.shape[0] // STRIPS
+    copies = []
+    for k, (src, dst) in enumerate(((hid, hid_out), (weights, w_out))):
+        for i in range(STRIPS):
+            at = pl.ds(i * strip, strip)
+            copies.append(pltpu.make_async_copy(src.at[at], dst.at[at], sem.at[k * STRIPS + i]))
+    for copy in copies:
+        copy.start()
+    for copy in copies:
+        copy.wait()
+
+
+def store(hid, weights):
+    anywhere, inside = pl.BlockSpec(memory_space=pl.ANY), pl.BlockSpec(memory_space=pltpu.VMEM)
+    hid = pltpu.with_memory_space_constraint(hid, pltpu.VMEM)
+    weights = pltpu.with_memory_space_constraint(weights, pltpu.VMEM)
+    return pl.pallas_call(
+        store_kernel,
+        out_shape=(
+            jax.ShapeDtypeStruct(hid.shape, hid.dtype),
+            jax.ShapeDtypeStruct(weights.shape, weights.dtype),
+        ),
+        in_specs=[inside, inside],
+        out_specs=(anywhere, anywhere),
+        scratch_shapes=[pltpu.SemaphoreType.DMA((2 * STRIPS,))],
+        compiler_params=pltpu.CompilerParams(vmem_limit_bytes=1000000),
+        name="store",
+    )(hid, weights)
 
 
 def grid_program(n_mp, radius, tokens, gain, weights, grads):
@@ -960,6 +1040,8 @@
             pltpu.VMEM((2, 128, 128), f32),
             pltpu.VMEM((n_mp, 2, count // 128, 8, 128), f32),
             pltpu.VMEM((8 * n_mp, 8, 128), f32),
+            pltpu.VMEM((rows // 2, CHUNK), bf16),
+            pltpu.VMEM((2, rows // 2, CHUNK), bf16),
             dma((2,)),
             dma((8 * SUBS,)),
             dma((2,)),
@@ -977,7 +1059,8 @@
             dma((16,)),
             dma((8,)),
         ]
-        + [dma((2,)), dma((pieces,))] * 4,
+        + [dma((2,)), dma((pieces,))] * 4
+        + [dma((3,))] * 2,
         compiler_params=pltpu.CompilerParams(
             collective_id=3, has_side_effects=True, vmem_limit_bytes=57000000
         ),
@@ -988,7 +1071,7 @@
 def per_device(n, n_mp, width, tokens, ln_gain, weights, grad_partials):
     radius = 0.7 * math.sqrt(width)
     if n == 4 and n_mp == 4 and weights.shape[1] % (8 * GROUP * CHUNK) == 0:
-        return grid_program(n_mp, radius, tokens, ln_gain, weights, grad_partials[0])
+        return store(*grid_program(n_mp, radius, tokens, ln_gain, weights, grad_partials[0]))
     return ring_program(n, n_mp, radius, tokens, ln_gain, weights, grad_partials)
 
 

time: 303 us -> 300 us (0.990)
  local copies, waits for them, and re-layouts: 4.37 us -> 0 us
    unnamed x2 -> x0, local copies, waits for them, and re-layouts: 4.37 us -> none
    pallas_call x0 -> x1, Pallas kernels: none -> 3.71 us  [store(): pl.pallas_call(store_kernel, out_shape=(jax.ShapeDtypeStruct(hid.shape, h...]
where the time goes in v3:
time: 300 us
  Pallas kernels  299 us (100%)
    pallas_call x1, Pallas kernels, grid_program(): pl.pallas_call(functools.partial(grid_kernel, n_mp, radius), out_shape=(p...  296 us

profile of v3, /device:TPU:0, one launch (start us, length us, event | category | flops | bytes accessed | tf_op | source)
XLA Modules:
  0.0 300.1 jit_solution(6031998356058887974)
XLA Ops:
  0.6 295.8 %grid_program.1 = (bf16[768,3072]{1,0:T(8,128)(2,1)S(1)}, bf16[768,3072]{1,0:T(8,128)(2,1)S(1)}) custom-call(bf16[768,1536]{1,0:T(8,128)(2,1)} %x_ref.1, bf16[1536]{0:T(1024)(128)(2,1)} %gain_ref.1, bf16[6144,3072]{1,0:T(8,128)(2,1)} %bitcast.1, bf16[768,3072]{1,0:T(8,128)(2,1)} %w_ref.1), custom_call_target="tpu_custom_call" | custom-call | tf_op jit(solution)/shard_map/grid_program/pallas_call | solution.py:1020
  296.4 3.7 %store.1 = (bf16[768,3072]{1,0:T(8,128)(2,1)}, bf16[768,3072]{1,0:T(8,128)(2,1)}) custom-call(bf16[768,3072]{1,0:T(8,128)(2,1)S(1)} %get-tuple-element.4.hid, bf16[768,3072]{1,0:T(8,128)(2,1)S(1)} %get-tuple-element.5.weights), custom_call_target="tpu_custom_call" | custom-call | tf_op jit(solution)/shard_map/store/pallas_call | solution.py:995

commit v4 on v3

--- a/solution.py
+++ b/solution.py
@@ -932,16 +932,31 @@
 
     spread_arrived(near_top + long_low + short_low)
     groups = (chunks[0] // GROUP, chunks[1] // GROUP)
-    turns = [0, 1] + [1 + GROUP * k for k in range(1, 2 * groups[0] - 1)]
+    turns = [0, 1] + [2 + GROUP * k for k in range(2 * groups[0] - 2)]
     spread_sent()
 
     @pl.loop(0, chunks[1])
     def _(j):
         arrive(1, j)
 
-        @pl.when(j > GROUP)
-        def _():
-            finish(1, j - GROUP - 1)
+        @pl.when((j % GROUP == 0) & (j > 0))
+        def _():
+            keep_near(1, j // GROUP - 1, 0)
+
+        @pl.when((j % GROUP == 1) & (j > 1))
+        def _():
+            keep_near(1, j // GROUP - 1, 1)
+
+        for k, turn in enumerate(turns):
+            @pl.when(j == turn)
+            def _():
+                keep_near(0, k // 2, k % 2)
+
+        send_far(1, j)
+
+        @pl.when(j >= GROUP + 2)
+        def _():
+            finish(1, j - GROUP - 2)
 
         for g in range(groups[0]):
             for k in range(GROUP):
@@ -949,25 +964,11 @@
                 def _():
                     finish(0, g * GROUP + k)
 
-        send_far(1, j)
-
-        @pl.when(j % GROUP == GROUP - 1)
-        def _():
-            keep_near(1, j // GROUP, 0)
-
-        @pl.when((j % GROUP == 0) & (j > 0))
-        def _():
-            keep_near(1, j // GROUP - 1, 1)
-
-        for k, turn in enumerate(turns):
-            @pl.when(j == turn)
-            def _():
-                keep_near(0, k // 2, k % 2)
-
-    keep_near(1, groups[1] - 1, 1)
+    for h in range(2):
+        keep_near(1, groups[1] - 1, h)
     for j in range(max(chunks[1] - turns[-1] - 1, 0), GROUP):
         finish(0, chunks[0] - GROUP + j)
-    for j in range(chunks[1] - GROUP - 1, chunks[1]):
+    for j in range(chunks[1] - GROUP - 2, chunks[1]):
         finish(1, j)
 
     head(2).wait_send()

time: 300 us -> 300 us (level)
  no operation moved by 1% of the time
where the time goes in v4:
time: 300 us
  Pallas kernels  299 us (100%)
    pallas_call x1, Pallas kernels, grid_program(): pl.pallas_call(functools.partial(grid_kernel, n_mp, radius), out_shape=(p...  296 us

profile of v4, /device:TPU:0, one launch (start us, length us, event | category | flops | bytes accessed | tf_op | source)
XLA Modules:
  0.0 300.1 jit_solution(12542912940076722014)
XLA Ops:
  0.6 295.8 %grid_program.1 = (bf16[768,3072]{1,0:T(8,128)(2,1)S(1)}, bf16[768,3072]{1,0:T(8,128)(2,1)S(1)}) custom-call(bf16[768,1536]{1,0:T(8,128)(2,1)} %x_ref.1, bf16[1536]{0:T(1024)(128)(2,1)} %gain_ref.1, bf16[6144,3072]{1,0:T(8,128)(2,1)} %bitcast.1, bf16[768,3072]{1,0:T(8,128)(2,1)} %w_ref.1), custom_call_target="tpu_custom_call" | custom-call | tf_op jit(solution)/shard_map/grid_program/pallas_call | solution.py:1021
  296.4 3.7 %store.1 = (bf16[768,3072]{1,0:T(8,128)(2,1)}, bf16[768,3072]{1,0:T(8,128)(2,1)}) custom-call(bf16[768,3072]{1,0:T(8,128)(2,1)S(1)} %get-tuple-element.4.hid, bf16[768,3072]{1,0:T(8,128)(2,1)S(1)} %get-tuple-element.5.weights), custom_call_target="tpu_custom_call" | custom-call | tf_op jit(solution)/shard_map/store/pallas_call | solution.py:996
